TPU v7x, 32 devices: a whole 2x2x4 slice. The times are simulated.
32 devices in a mesh: days: 4 (over y, x), space: 8 (over z, core).
Axes of the slice: x: 2, y: 2, z: 4, core: 2. Of those that a mesh axis runs over, the one named last changes fastest.
Arguments:
- fields: bfloat16 [640, 32, 1440], P('days', 'space')
- month_label: int32 [640], P('days'), may hold values from 0 to 11, as said below
- row_index: int32 [32], P('space'), may hold values from 0 to 31
- area_table: float32 [32], replicated, may hold values from 0.05 to 1
- basis: bfloat16 [64, 32, 1440], P(None, 'space'), may hold values from -6 to 6
Outputs:
- eofs: float32 [64, 32, 1440], P(None, 'space')
- pcs: float32 [640, 64], P('days')
Inputs may be any that keep to these rules, and one draw needn't show every extreme that they name: `month_label`: each day's label differs from floor(12 * day / 640) by at most one; the first day with a given value of floor(12 * day / 640) carries exactly that value; every month labels at least one day.
All inputs are finite; a program needn't handle non-finite values.
Results may differ from a plain program's by a relative error of at most 0.0003.
Values sent between devices are 32-bit elements; how exact they have to be, the bound alone decides.
A program may use at most 64 MiB of HBM per device.

v0:
```python
import jax
import jax.numpy as jnp
from jax import lax
from jax.sharding import PartitionSpec as P

ITERS = 2


HIGH = lax.Precision.HIGHEST


def solve_lower(lower, cover):
    shape = cover.shape
    solved = lax.linalg.triangular_solve(
        lower, cover.reshape(shape[0], -1), left_side=True, lower=True
    )
    return solved.reshape(shape)


def self_gram(cover):
    return jnp.einsum("klc,jlc->kj", cover, cover, precision=HIGH)


def local(fields, month_label, row_index, area_table, basis):
    months = jnp.arange(12, dtype=jnp.int32)
    onehot = (month_label[None, :] == months[:, None]).astype(jnp.bfloat16)
    sums = jnp.einsum("md,dlc->mlc", onehot, fields, preferred_element_type=jnp.float32)
    counts = jnp.sum(onehot.astype(jnp.float32), axis=1)
    sums, counts = lax.psum((sums, counts), "days")
    climate = sums / counts[:, None, None]
    seasonal = jnp.einsum("md,mlc->dlc", onehot.astype(jnp.float32), climate, precision=HIGH)
    table_hot = (
        row_index[:, None] == jnp.arange(area_table.shape[0], dtype=jnp.int32)[None, :]
    ).astype(jnp.float32)
    scale = jnp.sqrt(jnp.dot(table_hot, area_table, precision=HIGH))
    weighted = (fields.astype(jnp.float32) - seasonal) * scale[None, :, None]
    days_total = fields.shape[0] * lax.axis_size("days")
    partial_pcs = jnp.einsum("dlc,klc->dk", weighted, basis.astype(jnp.float32), precision=HIGH)
    pcs = lax.psum(partial_pcs, "space")
    eofs = basis.astype(jnp.float32)
    for step_count in range(ITERS):
        partial_cover = jnp.einsum("dk,dlc->klc", pcs, weighted, precision=HIGH) / days_total
        cover = lax.psum(partial_cover, "days")
        partial_gram = self_gram(cover)
        partial_raw = jnp.einsum("dlc,klc->dk", weighted, cover, precision=HIGH)
        gram, raw_pcs = lax.psum((partial_gram, partial_raw), "space")
        lower = jnp.linalg.cholesky(gram)
        eofs = solve_lower(lower, cover)
        pcs = lax.linalg.triangular_solve(
            lower, raw_pcs, left_side=False, lower=True, transpose_a=True
        )
    return (eofs, pcs)


def solution(mesh):
    placed = (P("days", "space", None), P("days"), P("space"), P(), P(None, "space", None))
    return jax.shard_map(
        local,
        mesh=mesh,
        in_specs=placed,
        out_specs=(P(None, "space", None), P("days", None)),
        check_vma=False,
    )
```

profile of v0, /device:TPU:0, one launch (start us, length us, event | category | flops | bytes accessed | tf_op | source)
XLA Modules:
  0.0 343.0 jit_solution(18154794807191105921)
XLA Ops:
  7.2 0.0 copy-start
  7.2 0.0 copy-start.5
  7.2 0.0 copy-start.4
  7.2 0.0 copy-start.7
  7.2 0.0 copy-start.6
  7.2 0.0 all-reduce.6.cloned.1.call-start
  7.3 3.1 fusion
  10.4 0.0 all-reduce.6.cloned.1.call-update
  10.4 0.0 all-reduce.8.cloned.1.call-start
  10.4 0.0 copy-done.5
  10.4 0.1 convert_reduce_fusion
  10.6 11.5 %psum.64 = f32[12]{0:T(128)S(1)} all-reduce(f32[12]{0:T(128)S(1)} %convert_reduce_fusion), channel_id=1, replica_groups=mesh['days'=4,'space'=8] {'days'}, use_global_device_ids=true, to_apply=%region_2.0 | all-reduce | flops 12 | bytes 96 | tf_op jit(solution)/shard_map/psum | solution.py:29
  22.0 0.0 copy-done.7
  22.0 0.0 copy-done.6
  22.1 0.2 fusion.4
  22.2 36.2 %all-reduce.6.cloned.1.call-done = f32[12,4,1440]{2,0,1:T(8,128)} async-done(((f32[12,4,1440]{2,0,1:T(8,128)}), f32[12,4,1440]{2,0,1:T(8,128)}) %all-reduce.6.cloned.1.call-update) | async-done | bytes 276496 | tf_op jit(solution)/shard_map/psum | solution.py:29
  58.4 0.0 copy-done.4
  58.4 3.2 subtract_multiply_fusion
  61.6 0.0 copy-start.1
  61.6 1.9 copy-done.1
  63.5 0.0 copy-done
  63.5 2.4 convolution_bitcast_fusion.4
  65.9 28.5 %psum.65 = f32[160,64]{0,1:T(8,128)S(1)} all-reduce(f32[160,64]{0,1:T(8,128)S(1)} %convolution_bitcast_fusion.4), channel_id=1, replica_groups=mesh['days'=4,'space'=8] {'space'}, use_global_device_ids=true, to_apply=%region_3.0 | all-reduce | flops 10240 | bytes 81920 | tf_op jit(solution)/shard_map/psum | solution.py:39
  94.4 5.4 %convolution_multiply_fusion.1 = f32[64,4,1440]{2,0,1:T(8,128)} fusion(f32[160,4,1440]{2,0,1:T(8,128)} %copy-done.1, f32[160,64]{0,1:T(8,128)S(1)} %psum.65), kind=kOutput, calls=%fused_computation.2 | convolution fusion | flops 708157440 | bytes 5201920 | tf_op jit(solution)/shard_map/dk,dlc->klc/dot_general | solution.py:42
  99.8 0.0 all-reduce.8.cloned.1.call-update
  99.8 0.2 all-reduce.10.cloned.1.call-start
  100.1 57.9 %all-reduce.8.cloned.1.call-done = f32[64,4,1440]{2,0,1:T(8,128)} async-done(((f32[64,4,1440]{2,0,1:T(8,128)}), f32[64,4,1440]{2,0,1:T(8,128)}) %all-reduce.8.cloned.1.call-update) | async-done | bytes 1474576 | tf_op jit(solution)/shard_map/psum | solution.py:43
  157.9 0.0 copy-start.3
  157.9 3.5 %convolution_bitcast_fusion.6 = f32[64,64]{0,1:T(8,128)S(1)} fusion(f32[64,4,1440]{2,0,1:T(8,128)} %all-reduce.8.cloned.1.call-done), kind=kOutput, calls=%fused_computation.13 | convolution fusion | flops 283115520 | bytes 1490944 | tf_op jit(solution)/shard_map/klc,jlc->kj/dot_general | solution.py:21
  161.4 0.0 copy-done.3
  161.4 5.3 %convolution_bitcast_fusion.1 = f32[160,64]{1,0:T(8,128)S(1)} fusion(f32[160,4,1440]{2,0,1:T(8,128)} %copy-done.1, f32[64,4,1440]{2,0,1:T(8,128)S(1)} %copy-done.3), kind=kOutput, calls=%fused_computation.8 | convolution fusion | flops 707788800 | bytes 5201920 | tf_op jit(solution)/shard_map/dlc,klc->dk/dot_general | solution.py:45
  166.7 29.8 %all-reduce.1 = (f32[160,64]{1,0:T(8,128)S(1)}, f32[64,64]{0,1:T(8,128)S(1)}) all-reduce(f32[160,64]{1,0:T(8,128)S(1)} %convolution_bitcast_fusion.1, f32[64,64]{0,1:T(8,128)S(1)} %convolution_bitcast_fusion.6), channel_id=1, replica_groups=mesh['days'=4,'space'=8] {'space'}, use_global_device_ids=true, to_apply=%region_8.0 | all-reduce | flops 14336 | bytes 114688 | tf_op jit(solution)/shard_map/psum | solution.py:46
  196.6 0.1 copy.16
  196.7 5.8 %cholesky.44 = f32[64,64]{1,0:T(8,128)S(1)} custom-call(f32[64,64]{1,0:T(8,128)S(1)} %fusion.15), custom_call_target="Cholesky" | custom-call | tf_op jit(solution)/shard_map/jit(cholesky)/cholesky | solution.py:47
  202.5 0.6 compare_reduce_fusion.1
  203.2 0.7 fusion.9
  203.8 4.9 %custom-call.10 = f32[1,64,64]{1,2,0:T(8,128)S(1)} custom-call(f32[1,64,64]{2,1,0:T(8,128)S(1)} %fusion.9), custom_call_target="InvertDiagBlocksLowerTriangular" | custom-call | tf_op jit(solution)/shard_map/triangular_solve/custom-call.0 | solution.py:49
  208.8 0.3 convolution_bitcast_fusion.3
  209.1 5.4 %convolution_multiply_fusion = f32[64,4,1440]{2,0,1:T(8,128)} fusion(f32[160,64,1]{0,1,2:T(8,128)S(1)} %convolution_bitcast_fusion.3, f32[160,4,1440]{2,0,1:T(8,128)} %copy-done.1), kind=kOutput, calls=%fused_computation.1 | convolution fusion | flops 708157440 | bytes 5201920 | tf_op jit(solution)/shard_map/dk,dlc->klc/dot_general | solution.py:42
  214.5 0.0 all-reduce.10.cloned.1.call-update
  214.5 58.1 %all-reduce.10.cloned.1.call-done = f32[64,4,1440]{2,0,1:T(8,128)} async-done(((f32[64,4,1440]{2,0,1:T(8,128)}), f32[64,4,1440]{2,0,1:T(8,128)}) %all-reduce.10.cloned.1.call-update) | async-done | bytes 1474576 | tf_op jit(solution)/shard_map/psum | solution.py:43
  272.6 3.6 %copy.19 = f32[64,4,1440]{2,1,0:T(4,128)} copy(f32[64,4,1440]{2,0,1:T(8,128)} %all-reduce.10.cloned.1.call-done) | data formatting | bytes 2949120 | tf_op jit(solution)/shard_map/psum | solution.py:43
  276.2 0.0 copy-start.2
  276.2 3.3 reshape.27
  279.5 0.0 copy-done.2
  279.5 5.3 %convolution_bitcast_fusion = f32[160,64]{1,0:T(8,128)S(1)} fusion(f32[160,4,1440]{2,0,1:T(8,128)} %copy-done.1, f32[64,4,1440]{2,0,1:T(8,128)S(1)} %copy-done.2), kind=kOutput, calls=%fused_computation.7 | convolution fusion | flops 707788800 | bytes 5201920 | tf_op jit(solution)/shard_map/dlc,klc->dk/dot_general | solution.py:45
  284.8 1.4 convolution_bitcast_fusion.5
  286.2 30.2 %all-reduce = (f32[64,64]{0,1:T(8,128)S(1)}, f32[160,64]{1,0:T(8,128)S(1)}) all-reduce(f32[64,64]{0,1:T(8,128)S(1)} %convolution_bitcast_fusion.5, f32[160,64]{1,0:T(8,128)S(1)} %convolution_bitcast_fusion), channel_id=1, replica_groups=mesh['days'=4,'space'=8] {'space'}, use_global_device_ids=true, to_apply=%region_10.13 | all-reduce | flops 14336 | bytes 114688 | tf_op jit(solution)/shard_map/psum | solution.py:46
  316.5 0.1 copy.18
  316.5 5.8 %cholesky.55 = f32[64,64]{1,0:T(8,128)S(1)} custom-call(f32[64,64]{1,0:T(8,128)S(1)} %fusion.13), custom_call_target="Cholesky" | custom-call | tf_op jit(solution)/shard_map/jit(cholesky)/cholesky | solution.py:47
  322.4 0.6 compare_reduce_fusion
  323.1 0.7 fusion.10
  323.7 4.9 %custom-call.8 = f32[1,64,64]{1,2,0:T(8,128)S(1)} custom-call(f32[1,64,64]{2,1,0:T(8,128)S(1)} %fusion.10), custom_call_target="InvertDiagBlocksLowerTriangular" | custom-call | tf_op jit(solution)/shard_map/triangular_solve | solution.py:14
  328.6 2.9 triangular_solve.34
  331.5 0.9 convolution_bitcast_fusion.2
  332.5 1.9 fusion.2
  334.4 2.2 copy.22
  (4 shorter events, 0.1 us)
Async XLA Ops:
  7.2 56.3 %copy-start = (bf16[64,4,1440]{2,1,0:T(4,128)(2,1)S(1)}, bf16[64,4,1440]{2,1,0:T(4,128)(2,1)}, u32[]{:S(2)}) copy-start(bf16[64,4,1440]{2,1,0:T(4,128)(2,1)} %param.12) | copy-start | bytes 2211844
  7.2 3.3 copy-start.5
  7.2 51.2 %copy-start.4 = (bf16[160,4,1440]{2,1,0:T(4,128)(2,1)S(1)}, bf16[160,4,1440]{2,1,0:T(4,128)(2,1)}, u32[]{:S(2)}) copy-start(bf16[160,4,1440]{2,1,0:T(4,128)(2,1)} %param.8) | copy-start | bytes 5529604
  7.2 14.8 %copy-start.7 = (f32[32]{0:T(128)S(1)}, f32[32]{0:T(128)}, u32[]{:S(2)}) copy-start(f32[32]{0:T(128)} %param.11) | copy-start | bytes 388
  7.2 14.8 %copy-start.6 = (s32[4]{0:T(128)S(1)}, s32[4]{0:T(128)}, u32[]{:S(2)}) copy-start(s32[4]{0:T(128)} %param.10) | copy-start | bytes 52
  7.2 51.2 %all-reduce.6.cloned.1.call-start = ((), (), s32[]{:S(2)}) async-start(), calls=%async_computation | async-start | bytes 786432 | tf_op jit(solution)/shard_map/psum | solution.py:29
  10.4 147.5 %all-reduce.8.cloned.1.call-start = ((), (), s32[]{:S(2)}) async-start(), calls=%async_computation.1 | async-start | bytes 3145728 | tf_op jit(solution)/shard_map/psum | solution.py:43
  61.6 1.9 copy-start.1
  99.8 172.8 %all-reduce.10.cloned.1.call-start = ((), (), s32[]{:S(2)}) async-start(), calls=%async_computation.2 | async-start | bytes 3145728 | tf_op jit(solution)/shard_map/psum | solution.py:43
  157.9 3.5 %copy-start.3 = (f32[64,4,1440]{2,0,1:T(8,128)S(1)}, f32[64,4,1440]{2,0,1:T(8,128)}, u32[]{:S(2)}) copy-start(f32[64,4,1440]{2,0,1:T(8,128)} %all-reduce.8.cloned.1.call-done) | copy-start | bytes 4423684
  276.2 3.3 copy-start.2
Sparse Core Ops, SparseCore 0:
  11.6 46.8 all-reduce.5
  99.9 57.9 all-reduce.7
  214.6 57.9 all-reduce.9
where the time goes:
time: 343 us
  waiting for transfers between devices  152 us (44%)
  blocking collectives  100 us (29%)
  matrix products  38.3 us (11%)
  other arithmetic  24.3 us (7%)
  local copies, waits for them, and re-layouts  14 us (4%)
  between operations  13.9 us (4%)
    psum x2, waiting for transfers between devices, local(): cover = lax.psum(partial_cover, 'days')  116 us
    psum x2, blocking collectives, local(): gram, raw_pcs = lax.psum((partial_gram, partial_raw), 'space')  60 us
    psum x1, waiting for transfers between devices, local(): sums, counts = lax.psum((sums, counts), 'days')  36.2 us
    psum x1, blocking collectives, local(): pcs = lax.psum(partial_pcs, 'space')  28.5 us
    another operation x6, other arithmetic, local(): lower = jnp.linalg.cholesky(gram)  13 us
    psum x1, blocking collectives, local(): sums, counts = lax.psum((sums, counts), 'days')  11.5 us
    dot_general x2, matrix products, local(): jnp.einsum('dk,dlc->klc', pcs, weighted, precision=HIGH) / days_total  10.8 us
    dot_general x2, matrix products, local(): partial_raw = jnp.einsum('dlc,klc->dk', weighted, cover, precision=HIGH)  10.6 us
  transfers between devices with their start and end apart: 3, of which 3 were waited for; matrix products, arithmetic and copies ran while one was open for 0% of the time, Pallas kernels for 0%

commit v1 on v0

v1 whole, which is shorter than its diff:
```python
import functools

import jax
import jax.numpy as jnp
from jax import lax
from jax.experimental import pallas as pl
from jax.experimental.pallas import tpu as pltpu
from jax.sharding import PartitionSpec as P

ITERS = 2
MESH = pl.DeviceIdType.MESH
HIGH = lax.Precision.HIGHEST
F32 = jnp.float32
BF16 = jnp.bfloat16
LANES = 128


def up(value, step):
    return -(-value // step) * step


def nt(a, b, **kw):
    return lax.dot_general(a, b, (((1,), (1,)), ((), ())), preferred_element_type=F32, **kw)


def nn(a, b, **kw):
    return lax.dot_general(a, b, (((1,), (0,)), ((), ())), preferred_element_type=F32, **kw)


def split3(x):
    high = x.astype(BF16)
    rest = x - high.astype(F32)
    mid = rest.astype(BF16)
    low = (rest - mid.astype(F32)).astype(BF16)
    return jnp.concatenate([high, mid, low], axis=0)


def join3(x, n):
    return x[:n] + (x[n : 2 * n] + x[2 * n :])


def inverse_factor(gram):
    n = gram.shape[0]
    sub = lax.broadcasted_iota(jnp.int32, (n, 1), 0)
    eye = (lax.broadcasted_iota(jnp.int32, (n, n), 0) == lax.broadcasted_iota(jnp.int32, (n, n), 1)).astype(F32)
    work = jnp.concatenate([gram, eye], axis=1)
    for j in range(n):
        row = work[j : j + 1, :]
        column = work[:, j : j + 1]
        inv = lax.rsqrt(work[j : j + 1, j : j + 1])
        row = row * inv
        work = jnp.where(sub == j, row, work - jnp.where(sub > j, column * inv, 0.0) * row)
    return work[:, n:]


def kernel(nd, ns, days_total, f_ref, b_ref, s_ref, e_ref, eofs_ref, pcs_ref,
           send_f, recv_f, full_f, p_part, p_rs, p_mine, p_all, q_all,
           x_out, x_rs, x_day, x_all, c_all, tall,
           sem_f, sem_prs, sem_pag, sem_pd, sem_xrs, sem_xd, sem_xag, sem_c):
    lat, dl, lon = f_ref.shape
    modes = eofs_ref.shape[1]
    rows = lat // nd
    day, space = lax.axis_index("days"), lax.axis_index("space")

    def peer(me, k, n):
        return lax.rem(me + k, n), lax.rem(me + n - k, n)

    def copy(src, dst, sems, index, axis, target):
        return pltpu.make_async_remote_copy(
            src_ref=src, dst_ref=dst, send_sem=sems.at[(0,) + index], recv_sem=sems.at[(1,) + index],
            device_id={axis: target}, device_id_type=MESH)

    barrier = pltpu.get_barrier_semaphore()
    for k in range(1, nd):
        pl.semaphore_signal(barrier, inc=1, device_id={"days": peer(day, k, nd)[0]}, device_id_type=MESH)
    for k in range(1, ns):
        pl.semaphore_signal(barrier, inc=1, device_id={"space": peer(space, k, ns)[0]}, device_id_type=MESH)
    pl.semaphore_wait(barrier, nd + ns - 2)

    f_sent = []
    for k in range(1, nd):
        to = peer(day, k, nd)[0]
        for r in range(rows):
            send_f[k - 1, r] = f_ref[to * rows + r].astype(F32)
        c = copy(send_f.at[k - 1], recv_f.at[day], sem_f, (k - 1,), "days", to)
        c.start()
        f_sent.append(c)

    total = None
    for l in range(lat):
        term = nt(f_ref[l], b_ref[l]) * s_ref[l]
        total = term if total is None else total + term
    height = p_part.shape[1]
    p_part[...] = jnp.zeros_like(p_part)
    for t in range(ns):
        have = min(dl, (t + 1) * height) - t * height
        if have > 0:
            p_part[t, :have] = total[t * height : t * height + have]
    sent = []
    for k in range(1, ns):
        to = peer(space, k, ns)[0]
        c = copy(p_part.at[to], p_rs.at[k - 1], sem_prs, (k - 1,), "space", to)
        c.start()
        sent.append(c)
    acc = p_part[space]
    for k in range(1, ns):
        sent[k - 1].wait()
        acc = acc + p_rs[k - 1]
    p_all[space] = acc
    sent = []
    for k in range(1, ns):
        to = peer(space, k, ns)[0]
        c = copy(p_all.at[space], p_all.at[space], sem_pag, (k - 1,), "space", to)
        c.start()
        sent.append(c)
    for k in range(1, ns):
        sent[k - 1].wait_send()
        frm = peer(space, k, ns)[1]
        copy(p_all.at[frm], p_all.at[frm], sem_pag, (k - 1,), "space", frm).wait_recv()
    p_mine[...] = jnp.concatenate([p_all[t] for t in range(ns)], axis=0)[:dl] + e_ref[...]
    sent = []
    q_all[day] = p_mine[...]
    for k in range(1, nd):
        to = peer(day, k, nd)[0]
        c = copy(p_mine, q_all.at[day], sem_pd, (k - 1,), "days", to)
        c.start()
        sent.append(c)
    for r in range(rows):
        full_f[r, pl.ds(pl.multiple_of(day * dl, 16), dl)] = f_ref[day * rows + r]
    for k in range(1, nd):
        sent[k - 1].wait_send()
        frm = peer(day, k, nd)[1]
        copy(p_mine, q_all.at[frm], sem_pd, (k - 1,), "days", frm).wait_recv()
    qt = jnp.concatenate([q_all[j] for j in range(nd)], axis=0).T
    start = qt[:modes]
    months = qt[LANES // 2 :] if modes <= LANES // 2 else qt[up(modes, LANES) :]
    mean_of = months / jnp.maximum(jnp.sum(months, axis=1, keepdims=True), 1.0)

    def center(x):
        return x - nn(nt(x, mean_of, precision=HIGH), months, precision=HIGH)

    pcs = center(start)
    for k in range(1, nd):
        f_sent[k - 1].wait_send()
        frm = peer(day, k, nd)[1]
        copy(send_f.at[k - 1], recv_f.at[frm], sem_f, (k - 1,), "days", frm).wait_recv()
        for r in range(rows):
            full_f[r, pl.ds(pl.multiple_of(frm * dl, 16), dl)] = recv_f[frm, r].astype(BF16)

    part = modes // ns
    n_days = nd * dl
    gram_at = up(n_days, LANES)
    for it in range(ITERS):
        last = it == ITERS - 1
        pcs3 = split3(pcs)
        gram, raw = None, None
        for r in range(rows):
            scale = s_ref[day * rows + r]
            cover = join3(nn(pcs3, full_f[r]), modes) * (scale * (1.0 / days_total))
            if last:
                c_all[day, r] = cover
            term = nt(cover, cover, precision=HIGH)
            gram = term if gram is None else gram + term
            term = join3(nt(split3(cover * scale), full_f[r]), modes)
            raw = term if raw is None else raw + term
        x_out[it, :, :n_days] = raw
        x_out[it, :, n_days:] = jnp.zeros((modes, x_out.shape[2] - n_days), F32)
        x_out[it, :, gram_at : gram_at + modes] = gram
        sent = []
        for k in range(1, ns):
            to = peer(space, k, ns)[0]
            c = copy(x_out.at[it, pl.ds(pl.multiple_of(to * part, part), part)], x_rs.at[it, k - 1],
                     sem_xrs, (it, k - 1), "space", to)
            c.start()
            sent.append(c)
        acc = x_out[it, pl.ds(pl.multiple_of(space * part, part), part)]
        for k in range(1, ns):
            sent[k - 1].wait()
            acc = acc + x_rs[it, k - 1]
        x_day[it, day] = acc
        sent = []
        for k in range(1, nd):
            to = peer(day, k, nd)[0]
            c = copy(x_day.at[it, day], x_day.at[it, day], sem_xd, (it, k - 1), "days", to)
            c.start()
            sent.append(c)
        c_sent = []
        if last:
            for k in range(1, nd):
                to = peer(day, k, nd)[0]
                c = copy(c_all.at[day], c_all.at[day], sem_c, (k - 1,), "days", to)
                c.start()
                c_sent.append(c)
        for k in range(1, nd):
            sent[k - 1].wait_send()
            frm = peer(day, k, nd)[1]
            copy(x_day.at[it, frm], x_day.at[it, frm], sem_xd, (it, k - 1), "days", frm).wait_recv()
        acc = x_day[it, 0]
        for j in range(1, nd):
            acc = acc + x_day[it, j]
        x_all[it, space] = acc
        sent = []
        for k in range(1, ns):
            to = peer(space, k, ns)[0]
            c = copy(x_all.at[it, space], x_all.at[it, space], sem_xag, (it, k - 1), "space", to)
            c.start()
            sent.append(c)
        for k in range(1, ns):
            sent[k - 1].wait_send()
            frm = peer(space, k, ns)[1]
            copy(x_all.at[it, frm], x_all.at[it, frm], sem_xag, (it, k - 1), "space", frm).wait_recv()
        whole = jnp.concatenate([x_all[it, t] for t in range(ns)], axis=0)
        inv = inverse_factor(whole[:, gram_at : gram_at + modes])
        raw = center(whole[:, :n_days])
        if not last:
            pcs = nn(inv, raw, precision=HIGH)
    tall[...] = raw.T
    mine = tall[pl.ds(pl.multiple_of(day * dl, 8), dl)]
    pcs_ref[...] = nt(mine, inv, precision=HIGH)
    for r in range(rows):
        eofs_ref[day * rows + r] = nn(inv, c_all[day, r], precision=HIGH)
    for k in range(1, nd):
        c_sent[k - 1].wait_send()
        frm = peer(day, k, nd)[1]
        copy(c_all.at[frm], c_all.at[frm], sem_c, (k - 1,), "days", frm).wait_recv()
        for r in range(rows):
            eofs_ref[frm * rows + r] = nn(inv, c_all[frm, r], precision=HIGH)


def solution(mesh):
    nd, ns = mesh.shape["days"], mesh.shape["space"]

    def local(fields, month_label, row_index, area_table, basis):
        dl, lat, lon = fields.shape
        modes = basis.shape[0]
        rows = lat // nd
        part = modes // ns
        group = up(modes, LANES // 2)
        wide = up(group + 12, LANES)
        height = up(-(-dl // ns), 8)
        n_days = nd * dl
        span = up(n_days, LANES) + up(modes, LANES)
        table_hot = (row_index[:, None] == jnp.arange(area_table.shape[0], dtype=jnp.int32)[None, :]).astype(F32)
        scale = jnp.sqrt(jnp.sum(table_hot * area_table[None, :], axis=1))
        extra = (month_label[:, None] == jnp.arange(wide, dtype=jnp.int32)[None, :] - group).astype(F32)
        f_t = jnp.transpose(fields, (1, 0, 2))
        b_t = jnp.pad(jnp.transpose(basis, (1, 0, 2)), ((0, 0), (0, wide - modes), (0, 0)))
        v, dma = pltpu.VMEM, pltpu.SemaphoreType.DMA
        eofs, pcs = pl.pallas_call(
            functools.partial(kernel, nd, ns, n_days),
            out_shape=(jax.ShapeDtypeStruct((lat, modes, lon), F32), jax.ShapeDtypeStruct((dl, modes), F32)),
            in_specs=[pl.BlockSpec(memory_space=v)] * 4,
            out_specs=(pl.BlockSpec(memory_space=v),) * 2,
            scratch_shapes=[
                v((nd - 1, rows, dl, lon), F32),
                v((nd, rows, dl, lon), F32),
                v((rows, n_days, lon), BF16),
                v((ns, height, wide), F32),
                v((ns - 1, height, wide), F32),
                v((dl, wide), F32),
                v((ns, height, wide), F32),
                v((nd, dl, wide), F32),
                v((ITERS, modes, span), F32),
                v((ITERS, ns - 1, part, span), F32),
                v((ITERS, nd, part, span), F32),
                v((ITERS, ns, part, span), F32),
                v((nd, rows, modes, lon), F32),
                v((n_days, modes), F32),
                dma((2, nd - 1)), dma((2, ns - 1)), dma((2, ns - 1)), dma((2, nd - 1)),
                dma((2, ITERS, ns - 1)), dma((2, ITERS, nd - 1)), dma((2, ITERS, ns - 1)), dma((2, nd - 1)),
            ],
            compiler_params=pltpu.CompilerParams(
                collective_id=0, has_side_effects=True, vmem_limit_bytes=60 * 1024 * 1024),
        )(f_t, b_t, jnp.broadcast_to(scale[:, None, None], (lat, 1, LANES))[:, :, :1], extra)
        return jnp.transpose(eofs, (1, 0, 2)), pcs

    placed = (P("days", "space", None), P("days"), P("space"), P(), P(None, "space", None))
    return jax.shard_map(
        local,
        mesh=mesh,
        in_specs=placed,
        out_specs=(P(None, "space", None), P("days", None)),
        check_vma=False,
    )
```

time: 343 us -> 123 us (0.36)
  waiting for transfers between devices: 152 us -> 0 us
  Pallas kernels: 0 us -> 110 us
  blocking collectives: 100 us -> 0 us
  matrix products: 38.3 us -> 0 us
  other arithmetic: 24.3 us -> 2.26 us
  between operations: 13.9 us -> 0.66 us
  local copies, waits for them, and re-layouts: 14 us -> 9.97 us
    psum x3 -> x0, waiting for transfers between devices: 152 us -> none  [the longest x2 116 us: local(): cover = lax.psum(partial_cover, 'days')]
    pallas_call x0 -> x1, Pallas kernels: none -> 110 us  [local(): pl.pallas_call(functools.partial(kernel, nd, ns, n_days), out_shape=(jax....]
    psum x4 -> x0, blocking collectives: 100 us -> none  [the longest x2 60 us: local(): gram, raw_pcs = lax.psum((partial_gram, partial_raw), 'space')]
    dot_general x10 -> x0, matrix products: 35.1 us -> none  [the longest x2 10.8 us: local(): jnp.einsum('dk,dlc->klc', pcs, weighted, precision=HIGH) / days_total]
    another operation x10 -> x0, other arithmetic: 24.2 us -> none  [the longest x6 13 us: local(): lower = jnp.linalg.cholesky(gram)]
    unnamed x17 -> x8, local copies, waits for them, and re-layouts: 4.06 us -> 8.03 us
    psum x3 -> x0, local copies, waits for them, and re-layouts: 3.71 us -> none  [the longest x1 3.56 us: local(): cover = lax.psum(partial_cover, 'days')]
  transfers between devices with their start and end apart: 3 -> 0, of which waited for: 3 -> 0; matrix products, arithmetic and copies ran while one was open for 0% -> 0% of each run, Pallas kernels for 0% -> 0%
where the time goes in v1:
time: 123 us
  Pallas kernels  110 us (89%)
  local copies, waits for them, and re-layouts  9.97 us (8%)
  other arithmetic  2.26 us (2%)
    pallas_call x1, Pallas kernels, local(): pl.pallas_call(functools.partial(kernel, nd, ns, n_days), out_shape=(jax....  110 us
    unnamed x8, local copies, waits for them, and re-layouts  8.03 us

profile of v1, /device:TPU:0, one launch (start us, length us, event | category | flops | bytes accessed | tf_op | source)
XLA Modules:
  0.0 122.7 jit_solution(16939974228469535308)
XLA Ops:
  0.6 0.9 select_reduce_fusion
  1.5 0.7 copy.14.s_ref
  2.2 1.4 %compare_convert_fusion.e_ref = f32[160,128]{1,0:T(8,128)} fusion(s32[128]{0:T(128)S(1)} %iota_add_fusion, s32[160]{0:T(256)} %param.6), kind=kLoop, calls=%fused_computation.2 | loop fusion | flops 40960 | bytes 83072 | tf_op jit(solution)/shard_map/convert_element_type | solution.py:245
  3.6 1.3 %copy.20 = bf16[64,4,1440]{2,0,1:T(8,128)(2,1)S(1)} copy(bf16[64,4,1440]{2,1,0:T(4,128)(2,1)} %param.9) | data formatting | bytes 1474560 | tf_op args[4]
  4.8 0.0 copy-start
  4.8 1.3 %pad.4.b_ref = bf16[4,128,1440]{2,1,0:T(8,128)(2,1)} pad(bf16[4,64,1440]{2,1,0:T(8,128)(2,1)S(1)} %bitcast.10, bf16[]{:T(256)} %constant.6.clone.1), padding=0_0x0_64x0_0 | pad | bytes 2211842 | tf_op jit(solution)/shard_map/jit(_pad)/pad | solution.py:247
  6.1 0.8 copy-done
  6.9 1.6 %copy.19 = bf16[160,4,1440]{2,0,1:T(8,128)(2,1)} copy(bf16[160,4,1440]{2,1,0:T(4,128)(2,1)S(1)} %copy-done) | data formatting | bytes 3686400 | tf_op args[0]
  8.6 109.8 %shard_map.68 = (f32[4,64,1440]{2,1,0:T(8,128)}, f32[160,64]{1,0:T(8,128)}) custom-call(bf16[4,160,1440]{2,1,0:T(8,128)(2,1)} %bitcast.9, bf16[4,128,1440]{2,1,0:T(8,128)(2,1)} %pad.4.b_ref, f32[4,1,1]{2,1,0:T(1,128)} %copy.14.s_ref, f32[160,128]{1,0:T(8,128)} %compare_convert_fusion.e_ref), custom_call_target="tpu_custom_call" | custom-call | tf_op jit(solution)/shard_map/pallas_call | solution.py:249
  118.4 0.0 copy-start.1
  118.4 3.6 %copy.15 = f32[64,4,1440]{2,1,0:T(4,128)} copy(f32[64,4,1440]{2,0,1:T(8,128)} %bitcast.11) | data formatting | bytes 2949120
  122.0 0.0 copy-done.1
  122.0 0.7 copy.16
  (2 shorter events, 0.0 us)
Async XLA Ops:
  4.8 2.1 %copy-start = (bf16[160,4,1440]{2,1,0:T(4,128)(2,1)S(1)}, bf16[160,4,1440]{2,1,0:T(4,128)(2,1)}, u32[]{:S(2)}) copy-start(bf16[160,4,1440]{2,1,0:T(4,128)(2,1)} %param.5) | copy-start | bytes 5529604
  118.4 3.6 %copy-start.1 = (f32[160,64]{1,0:T(8,128)S(1)}, f32[160,64]{1,0:T(8,128)}, u32[]{:S(2)}) copy-start(f32[160,64]{1,0:T(8,128)} %get-tuple-element.9) | copy-start | bytes 122884

commit v2 on v1

--- a/solution.py
+++ b/solution.py
@@ -53,17 +53,23 @@
     return work[:, n:]
 
 
-def kernel(nd, ns, days_total, f_ref, b_ref, s_ref, e_ref, eofs_ref, pcs_ref,
+def kernel(nd, ns, days_total, f_ref, b_ref, i_ref, a_ref, l_ref, eofs_ref, pcs_ref,
            send_f, recv_f, full_f, p_part, p_rs, p_mine, p_all, q_all,
-           x_out, x_rs, x_day, x_all, c_all, tall,
+           x_out, x_rs, x_day, x_all, c_all, tall, s_ref,
            sem_f, sem_prs, sem_pag, sem_pd, sem_xrs, sem_xd, sem_xag, sem_c):
     lat, dl, lon = f_ref.shape
-    modes = eofs_ref.shape[1]
+    modes = eofs_ref.shape[0]
     rows = lat // nd
     day, space = lax.axis_index("days"), lax.axis_index("space")
 
     def peer(me, k, n):
-        return lax.rem(me + k, n), lax.rem(me + n - k, n)
+        if n & (n - 1):
+            return lax.rem(me + k, n), lax.rem(me + n - k, n)
+        other = me
+        for bit in range(n.bit_length()):
+            if (k >> bit) & 1:
+                other = other + (1 << bit) * (1 - 2 * lax.rem(lax.div(me, 1 << bit), 2))
+        return other, other
 
     def copy(src, dst, sems, index, axis, target):
         return pltpu.make_async_remote_copy(
@@ -78,7 +84,8 @@
     pl.semaphore_wait(barrier, nd + ns - 2)
 
     f_sent = []
-    for k in range(1, nd):
+
+    def send_fields(k):
         to = peer(day, k, nd)[0]
         for r in range(rows):
             send_f[k - 1, r] = f_ref[to * rows + r].astype(F32)
@@ -86,11 +93,18 @@
         c.start()
         f_sent.append(c)
 
+    for k in range(1, nd - 1):
+        send_fields(k)
+    scales = [jnp.sqrt(jnp.full((1, 1), a_ref[i_ref[l]], F32)) for l in range(lat)]
+    for l in range(lat):
+        s_ref[l] = scales[l]
+
     total = None
     for l in range(lat):
-        term = nt(f_ref[l], b_ref[l]) * s_ref[l]
+        term = nt(f_ref[l], b_ref[:, l, :]) * scales[l]
         total = term if total is None else total + term
-    height = p_part.shape[1]
+    height, wide = p_part.shape[1:]
+    total = jnp.concatenate([total, jnp.zeros((dl, wide - modes), F32)], axis=1)
     p_part[...] = jnp.zeros_like(p_part)
     for t in range(ns):
         have = min(dl, (t + 1) * height) - t * height
@@ -117,7 +131,9 @@
         sent[k - 1].wait_send()
         frm = peer(space, k, ns)[1]
         copy(p_all.at[frm], p_all.at[frm], sem_pag, (k - 1,), "space", frm).wait_recv()
-    p_mine[...] = jnp.concatenate([p_all[t] for t in range(ns)], axis=0)[:dl] + e_ref[...]
+    group = up(modes, LANES // 2)
+    hot = (l_ref[...] == lax.broadcasted_iota(jnp.int32, (wide, dl), 0) - group).astype(F32)
+    p_mine[...] = jnp.concatenate([p_all[t] for t in range(ns)], axis=0)[:dl] + hot.T
     sent = []
     q_all[day] = p_mine[...]
     for k in range(1, nd):
@@ -125,6 +141,7 @@
         c = copy(p_mine, q_all.at[day], sem_pd, (k - 1,), "days", to)
         c.start()
         sent.append(c)
+    send_fields(nd - 1)
     for r in range(rows):
         full_f[r, pl.ds(pl.multiple_of(day * dl, 16), dl)] = f_ref[day * rows + r]
     for k in range(1, nd):
@@ -216,15 +233,14 @@
             pcs = nn(inv, raw, precision=HIGH)
     tall[...] = raw.T
     mine = tall[pl.ds(pl.multiple_of(day * dl, 8), dl)]
-    pcs_ref[...] = nt(mine, inv, precision=HIGH)
-    for r in range(rows):
-        eofs_ref[day * rows + r] = nn(inv, c_all[day, r], precision=HIGH)
+    pcs_ref[...] = nt(inv, mine, precision=HIGH)
     for k in range(1, nd):
         c_sent[k - 1].wait_send()
         frm = peer(day, k, nd)[1]
         copy(c_all.at[frm], c_all.at[frm], sem_c, (k - 1,), "days", frm).wait_recv()
-        for r in range(rows):
-            eofs_ref[frm * rows + r] = nn(inv, c_all[frm, r], precision=HIGH)
+    for j in range(nd):
+        for r in range(rows):
+            eofs_ref[:, j * rows + r, :] = nn(inv, c_all[j, r], precision=HIGH)
 
 
 def solution(mesh):
@@ -240,16 +256,13 @@
         height = up(-(-dl // ns), 8)
         n_days = nd * dl
         span = up(n_days, LANES) + up(modes, LANES)
-        table_hot = (row_index[:, None] == jnp.arange(area_table.shape[0], dtype=jnp.int32)[None, :]).astype(F32)
-        scale = jnp.sqrt(jnp.sum(table_hot * area_table[None, :], axis=1))
-        extra = (month_label[:, None] == jnp.arange(wide, dtype=jnp.int32)[None, :] - group).astype(F32)
         f_t = jnp.transpose(fields, (1, 0, 2))
-        b_t = jnp.pad(jnp.transpose(basis, (1, 0, 2)), ((0, 0), (0, wide - modes), (0, 0)))
         v, dma = pltpu.VMEM, pltpu.SemaphoreType.DMA
         eofs, pcs = pl.pallas_call(
             functools.partial(kernel, nd, ns, n_days),
-            out_shape=(jax.ShapeDtypeStruct((lat, modes, lon), F32), jax.ShapeDtypeStruct((dl, modes), F32)),
-            in_specs=[pl.BlockSpec(memory_space=v)] * 4,
+            out_shape=(jax.ShapeDtypeStruct((modes, lat, lon), F32), jax.ShapeDtypeStruct((modes, dl), F32)),
+            in_specs=[pl.BlockSpec(memory_space=v)] * 2 + [pl.BlockSpec(memory_space=pltpu.SMEM)] * 2
+            + [pl.BlockSpec(memory_space=v)],
             out_specs=(pl.BlockSpec(memory_space=v),) * 2,
             scratch_shapes=[
                 v((nd - 1, rows, dl, lon), F32),
@@ -266,13 +279,14 @@
                 v((ITERS, ns, part, span), F32),
                 v((nd, rows, modes, lon), F32),
                 v((n_days, modes), F32),
+                v((lat, 1, 1), F32),
                 dma((2, nd - 1)), dma((2, ns - 1)), dma((2, ns - 1)), dma((2, nd - 1)),
                 dma((2, ITERS, ns - 1)), dma((2, ITERS, nd - 1)), dma((2, ITERS, ns - 1)), dma((2, nd - 1)),
             ],
             compiler_params=pltpu.CompilerParams(
                 collective_id=0, has_side_effects=True, vmem_limit_bytes=60 * 1024 * 1024),
-        )(f_t, b_t, jnp.broadcast_to(scale[:, None, None], (lat, 1, LANES))[:, :, :1], extra)
-        return jnp.transpose(eofs, (1, 0, 2)), pcs
+        )(f_t, basis, row_index, area_table, month_label[None, :])
+        return eofs, pcs.T
 
     placed = (P("days", "space", None), P("days"), P("space"), P(), P(None, "space", None))
     return jax.shard_map(

time: 123 us -> 115 us (0.935)
  local copies, waits for them, and re-layouts: 9.97 us -> 6.48 us
  other arithmetic: 2.26 us -> 0 us
  Pallas kernels: 110 us -> 108 us
    pallas_call x1, Pallas kernels: 110 us -> 108 us  [local(): pl.pallas_call(functools.partial(kernel, nd, ns, n_days), out_shape=(jax....]
    unnamed x8 -> x5, local copies, waits for them, and re-layouts: 8.03 us -> 6.48 us
    convert_element_type x1 -> x0, other arithmetic: 1.4 us -> none  [local(): (month_label[:, None] == jnp.arange(wide, dtype=jnp.int32)[None, :] - gro...]
    pad x1 -> x0, local copies, waits for them, and re-layouts: 1.26 us -> none  [local(): jnp.pad(jnp.transpose(basis, (1, 0, 2)), ((0, 0), (0, wide - modes), (0,...]
where the time goes in v2:
time: 115 us
  Pallas kernels  108 us (94%)
  local copies, waits for them, and re-layouts  6.48 us (6%)
    pallas_call x1, Pallas kernels, local(): pl.pallas_call(functools.partial(kernel, nd, ns, n_days), out_shape=(jax....  108 us
    unnamed x5, local copies, waits for them, and re-layouts  6.48 us

profile of v2, /device:TPU:0, one launch (start us, length us, event | category | flops | bytes accessed | tf_op | source)
XLA Modules:
  0.0 115.1 jit_solution(360879041262705176)
XLA Ops:
  0.6 3.2 %copy.9 = bf16[160,4,1440]{2,0,1:T(8,128)(2,1)} copy(bf16[160,4,1440]{2,1,0:T(4,128)(2,1)} %param.5) | data formatting | bytes 3686400 | tf_op args[0]
  3.8 108.0 %shard_map.68 = (f32[64,4,1440]{2,1,0:T(4,128)}, f32[64,160]{1,0:T(8,128)}) custom-call(bf16[4,160,1440]{2,1,0:T(8,128)(2,1)} %bitcast.5, bf16[64,4,1440]{2,1,0:T(4,128)(2,1)} %b_ref.1, s32[4]{0:T(128)} %i_ref.1, f32[32]{0:T(128)} %a_ref.1, s32[1,160]{1,0:T(1,128)} %bitcast.7), custom_call_target="tpu_custom_call" | custom-call | tf_op jit(solution)/shard_map/pallas_call | solution.py:261
  111.8 0.0 copy-start
  111.8 2.7 %copy.12 = f32[64,4,1440]{2,1,0:T(4,128)} copy(f32[64,4,1440]{2,1,0:T(4,128)} %get-tuple-element.8) | data formatting | bytes 2949120
  114.5 0.0 copy-done
  114.5 0.6 copy.13
Async XLA Ops:
  111.8 2.7 %copy-start = (f32[64,160]{1,0:T(8,128)S(1)}, f32[64,160]{1,0:T(8,128)}, u32[]{:S(2)}) copy-start(f32[64,160]{1,0:T(8,128)} %get-tuple-element.5) | copy-start | bytes 122884
